TPU v7x, 256 devices: a whole 4x4x8 slice. The times are simulated.
256 devices in a mesh: dp: 32 (over x_lo, z, core), mp: 8 (over x_hi, y).
Axes of the slice: x: 4 (x_hi: 2, x_lo: 2; x = x_hi * 2 + x_lo), y: 4, z: 8, core: 2. Of those that a mesh axis runs over, the one named last changes fastest.
Arguments:
- token_ids: int32 [32, 512], P('dp', 'mp'), may hold values from 0 to 128255
- embedding: bfloat16 [128256, 8192], P('mp', 'dp'), may hold values from -6 to 6
- norm_gain: bfloat16 [8192], replicated, may hold values from 0.099609375 to 1.8984375
- query_weight: bfloat16 [8192, 4096], P('dp', 'mp'), may hold values from -4 to 4
- key_weight: bfloat16 [8192, 1024], P('dp', 'mp'), may hold values from -0.0625 to 0.0625
- value_weight: bfloat16 [8192, 1024], P('dp', 'mp'), may hold values from -0.0625 to 0.0625
Outputs:
- attention: bfloat16 [16384, 4096], P('dp', 'mp')
All inputs are finite; a program needn't handle non-finite values.
Results may differ from a plain program's by a relative error of at most 0.0095.
The roundings to bfloat16 on the way count: a program that leaves them out, or rounds other values in their place, can miss the bound.
Values may be sent and summed in bfloat16 or wider, within the bound.
No kernel may reach another device: no remote copies, remote signals or barrier semaphores. Data moves between devices by JAX's collectives and lax.ppermute only.
A program may use at most 128 MiB of HBM per device.

v0:
```python
import jax
import jax.numpy as jnp
from jax import lax
from jax.sharding import Mesh
from jax.sharding import PartitionSpec as P

HD = 128
MP = ("mp_0", "mp_1")
DP_MP = ("dp", "mp_0", "mp_1")
rope_base = 500000.0
epsilon = 1e-05


def reduced_to_own(tiles, axes, order):
    shape = [lax.axis_size(a) for a in axes]
    tiles = tiles.reshape(*shape, *tiles.shape[1:])
    tiles = tiles.transpose(*order, *range(len(axes), tiles.ndim))
    tiles = tiles.reshape(-1, *tiles.shape[len(axes) :])
    for k in order:
        tiles = lax.psum_scatter(tiles, axes[k], scatter_dimension=0, tiled=True)
    return tiles[0]


def in_blocks(array, dim, size):
    shape = array.shape
    tiles = array.reshape(*shape[:dim], size, shape[dim] // size, *shape[dim + 1 :])
    return jnp.moveaxis(tiles, dim, 0)


def scatter_axes(array, axes, order, dim):
    size = lax.axis_size(axes)
    return reduced_to_own(in_blocks(array, dim, size), axes, order)


def side_by_side(arrays, axis, dim, along):
    both = jnp.concatenate(arrays, axis=along)
    whole, at, outs = (lax.all_gather(both, axis, axis=dim, tiled=True), 0, [])
    for a in arrays:
        outs.append(lax.slice_in_dim(whole, at, at + a.shape[along], axis=along))
        at += a.shape[along]
    return tuple(outs)


def normalize(values, norm_gain):
    factor = lax.rsqrt(jnp.mean(values * values, axis=-1, keepdims=True) + epsilon)
    return (values * factor * norm_gain.astype(jnp.float32)).astype(jnp.bfloat16)


def rotate(values, positions):
    half_width = values.shape[-1] // 2
    frequency = rope_base ** (-(jnp.arange(half_width, dtype=jnp.float32) * 2.0) / values.shape[-1])
    angles = (positions[:, None] * frequency[None, :])[:, None, :]
    cosine = jnp.cos(angles)
    sine_wave = jnp.sin(angles)
    first_half = values[..., :half_width]
    second_half = values[..., half_width:]
    return jnp.concatenate(
        [
            first_half * cosine - second_half * sine_wave,
            second_half * cosine + first_half * sine_wave,
        ],
        axis=-1,
    )


def attend(queries, key_block, value_block):
    length = queries.shape[0]
    scores = jnp.einsum(
        "skgd,tkd->kgst", queries, key_block, preferred_element_type=jnp.float32
    ) * queries.shape[-1] ** (-0.5)
    causal = jnp.arange(length)[:, None] >= jnp.arange(length)[None, :]
    scores = jnp.where(causal, scores, -jnp.inf)
    highest = jnp.max(scores, axis=-1, keepdims=True)
    raised = jnp.exp(scores - highest)
    weights = (raised / jnp.sum(raised, axis=-1, keepdims=True)).astype(jnp.bfloat16)
    blended = jnp.einsum("kgst,tkd->skgd", weights, value_block, preferred_element_type=jnp.float32)
    return blended.reshape(length, -1).astype(jnp.bfloat16)


def per_device(token_ids, embedding, norm_gain, query_weight, key_weight, value_weight):
    responses, span = token_ids.shape
    vocab_rows = embedding.shape[0]
    dp_count = lax.axis_size("dp")
    mp_count = lax.axis_size(MP)
    length = span * mp_count
    flat_ids = token_ids.reshape(responses * span)
    every_id = lax.all_gather(flat_ids, DP_MP, axis=0, tiled=True)
    ordered = every_id.reshape(dp_count, mp_count, responses, span).transpose(0, 2, 1, 3)
    local_ids = ordered - lax.axis_index(MP) * vocab_rows
    inside = (local_ids >= 0) & (local_ids < vocab_rows)
    looked = jnp.take(embedding, jnp.clip(local_ids, 0, vocab_rows - 1), axis=0)
    looked = jnp.where(inside[..., None], looked, jnp.zeros((), jnp.bfloat16))
    shared = scatter_axes(looked, MP, (1, 0), 2).astype(jnp.float32)
    moved = lax.all_to_all(
        shared.astype(jnp.bfloat16), "dp", split_axis=0, concat_axis=4, tiled=True
    )
    share_normed = normalize(moved.astype(jnp.float32).reshape(responses, span, -1), norm_gain)
    normed = lax.all_gather(share_normed, MP, axis=1, tiled=True)
    flat_normed = normed.reshape(responses * length, -1)

    def project(piece):
        return jnp.dot(flat_normed, piece, preferred_element_type=jnp.float32)

    pieces = side_by_side((query_weight, key_weight, value_weight), "dp", 0, 1)
    query_proj = project(pieces[0])
    key_proj = project(pieces[1])
    value_proj = project(pieces[2])
    heads_here = query_weight.shape[1] // HD
    kv_here = key_weight.shape[1] // HD
    positions = jnp.arange(length, dtype=jnp.float32)
    queries = rotate(query_proj.reshape(responses, length, heads_here, HD), positions).astype(
        jnp.bfloat16
    )
    queries = queries.reshape(responses, length, kv_here, heads_here // kv_here, HD)
    key_block = rotate(key_proj.reshape(responses, length, kv_here, HD), positions).astype(
        jnp.bfloat16
    )
    value_block = value_proj.reshape(responses, length, kv_here, HD).astype(jnp.bfloat16)
    output = lax.map(
        lambda group: attend(group[0], group[1], group[2]), (queries, key_block, value_block)
    )
    return output.reshape(responses * length, heads_here * HD)


def solution(mesh):
    split = Mesh(mesh.devices.reshape(mesh.shape["dp"], 2, 4), ("dp", "mp_0", "mp_1"))
    in_specs = (P("dp", MP), P(MP, "dp"), P(), P("dp", MP), P("dp", MP), P("dp", MP))
    out_specs = P("dp", MP)
    return jax.shard_map(
        per_device, mesh=split, in_specs=in_specs, out_specs=out_specs, check_vma=False
    )
```

profile of v0, /device:TPU:1, one launch (start us, length us, event | category | flops | bytes accessed | tf_op | source)
XLA Modules:
  0.0 695.4 jit_solution(9805546646398294829)
XLA Ops:
  7.4 0.8 bitcast_dynamic-update-slice_fusion
  8.1 0.6 copy-done.3
  8.8 0.0 all-reduce.3.cloned.1.call-update
  8.8 0.0 reduce-scatter.3.cloned.1.call-start
  8.9 250.5 %all-reduce.3.cloned.1.call-done = s32[16384]{0:T(1024)} async-done(((s32[16384]{0:T(1024)}), s32[16384]{0:T(1024)}) %all-reduce.3.cloned.1.call-update) | async-done | bytes 65552
  259.3 0.9 subtract_clamp_fusion
  260.2 0.1 min.18
  260.3 0.1 min.16
  260.4 0.1 reshape.370
  260.5 0.9 compare_and_fusion.1
  261.4 0.1 and.23
  261.5 65.6 %gather_fusion = bf16[16384,256]{1,0:T(8,128)(2,1)} fusion(bf16[16032,256]{1,0:T(8,128)(2,1)} %param.7, s32[16384]{0:T(1024)S(1)} %broadcast_clamp_fusion), kind=kCustom, calls=%fused_computation | custom fusion | bytes 16842752 | tf_op jit(solution)/shard_map/jit(_take)/gather | solution.py:91
  327.1 7.7 %select_select_fusion = bf16[32,1,8,1,64,256]{5,4,2,0,3,1:T(8,128)(2,1)} fusion(bf16[32,1,8,1,64,256]{5,4,2,0,3,1:T(8,128)(2,1)} %bitcast.88, pred[32,8,64]{2,1,0:T(8,128)(4,1)S(1)} %compare_and_fusion, pred[32,8,64]{2,1,0:T(8,128)(4,1)S(1)} %and.23), kind=kLoop, calls=%fused_computation.8 | loop fusion | flops 8388608 | bytes 16809984 | tf_op jit(solution)/shard_map/jit(_where)/select_n | solution.py:92
  334.8 8.3 %copy.19 = bf16[2,4,32,1,1,64,256]{6,5,2,0,1,4,3:T(8,128)(2,1)} copy(bf16[2,4,32,1,1,64,256]{6,5,1,0,2,4,3:T(8,128)(2,1)} %bitcast.90) | data formatting | bytes 16777216 | tf_op jit(solution)/shard_map/reshape | solution.py:16
  343.1 0.0 reduce-scatter.3.cloned.1.call-update
  343.1 0.0 copy-start.6
  343.1 0.0 reduce-scatter.5.cloned.1.call-start
  343.2 79.3 %reduce-scatter.3.cloned.1.call-done = bf16[2,32,1,1,64,256]{5,4,1,3,2,0:T(8,128)(2,1)} async-done(((bf16[8,32,1,1,64,256]{5,4,1,3,2,0:T(8,128)(2,1)}), bf16[2,32,1,1,64,256]{5,4,1,3,2,0:T(8,128)(2,1)}) %reduce-scatter.3.cloned.1.call-update) | async-done | bytes 2097168 | tf_op jit(solution)/shard_map/reduce_scatter | solution.py:20
  422.5 0.0 reduce-scatter.5.cloned.1.call-update
  422.5 0.0 all-gather.6.cloned.1.call-start
  422.5 0.0 copy-done.2
  422.6 0.8 pad_maximum_fusion
  423.3 0.0 all-gather.6.cloned.1.call-update
  423.4 39.8 %reduce-scatter.5.cloned.1.call-done = bf16[1,32,1,1,64,256]{5,4,1,3,2,0:T(8,128)(2,1)} async-done(((bf16[2,32,1,1,64,256]{5,4,1,3,2,0:T(8,128)(2,1)}), bf16[1,32,1,1,64,256]{5,4,1,3,2,0:T(8,128)(2,1)}) %reduce-scatter.5.cloned.1.call-update) | async-done | bytes 1048592 | tf_op jit(solution)/shard_map/reduce_scatter | solution.py:20
  463.1 8.0 %all-to-all-start = ((bf16[32,1,1,64,256]{4,3,2,1,0:T(8,128)(2,1)}), bf16[32,1,1,64,256]{4,3,2,1,0:T(8,128)(2,1)S(1)}, u32[]{:S(2)}, u32[]{:S(2)}) async-start(bf16[32,1,1,64,256]{4,3,2,1,0:T(8,128)(2,1)} %bitcast.92), calls=%async_computation.2 | async-start | bytes 2097152 | tf_op jit(solution)/shard_map/all_to_all | solution.py:94
  471.1 0.2 all-gather.4.cloned.1.call-start
  471.4 37.2 %all-to-all-done = bf16[32,1,1,64,256]{4,3,2,1,0:T(8,128)(2,1)S(1)} async-done(((bf16[32,1,1,64,256]{4,3,2,1,0:T(8,128)(2,1)}), bf16[32,1,1,64,256]{4,3,2,1,0:T(8,128)(2,1)S(1)}, u32[]{:S(2)}, u32[]{:S(2)}) %all-to-all-start) | async-done | bytes 1048608 | tf_op jit(solution)/shard_map/all_to_all | solution.py:94
  508.6 0.3 convert_bitcast_fusion
  508.9 2.5 copy.20
  511.5 1.8 reshape.366
  513.2 0.3 fusion.8
  513.5 1.3 multiply_convert_fusion
  514.8 0.0 all-gather.4.cloned.1.call-update
  514.8 0.1 iota_compare_fusion
  514.9 0.5 fusion.48
  515.5 31.8 %all-gather.6.cloned.1.call-done = bf16[8192,768]{1,0:T(8,128)(2,1)} async-done(((bf16[256,768]{1,0:T(8,128)(2,1)}), bf16[8192,768]{1,0:T(8,128)(2,1)}) %all-gather.6.cloned.1.call-update) | async-done | bytes 12582928 | tf_op jit(solution)/shard_map/all_gather | solution.py:37
  547.2 7.4 %slice_bitcast_fusion = bf16[512,8192]{0,1:T(8,128)(2,1)} fusion(bf16[8192,768]{1,0:T(8,128)(2,1)} %all-gather.6.cloned.1.call-done), kind=kLoop, calls=%fused_computation.1 | loop fusion | bytes 16777216 | tf_op jit(solution)/shard_map/dot_general | solution.py:102
  554.6 12.0 %copy.21 = bf16[512,8192]{1,0:T(8,128)(2,1)} copy(bf16[512,8192]{0,1:T(8,128)(2,1)} %slice_bitcast_fusion) | data formatting | bytes 16777216 | tf_op jit(solution)/shard_map/dot_general | solution.py:102
  566.6 93.0 %all-gather.4.cloned.1.call-done = bf16[1,512,8192]{2,1,0:T(8,128)(2,1)} async-done(((bf16[1,64,8192]{2,1,0:T(8,128)(2,1)}), bf16[1,512,8192]{2,1,0:T(8,128)(2,1)}) %all-gather.4.cloned.1.call-update) | async-done | bytes 8388624 | tf_op jit(solution)/shard_map/all_gather | solution.py:98
  659.5 7.0 %fusion.20 = f32[1,512,1,128]{1,3,2,0:T(8,128)S(1)} fusion(bf16[8192,768]{1,0:T(8,128)(2,1)} %all-gather.6.cloned.1.call-done, bf16[1,512,8192]{2,1,0:T(8,128)(2,1)} %all-gather.4.cloned.1.call-done), kind=kOutput, calls=%fused_computation.25 | convolution fusion | flops 1073741824 | bytes 10747904 | tf_op jit(solution)/shard_map/dot_general | solution.py:102
  666.6 0.6 fusion.51
  667.1 7.2 %fusion.14 = f32[1,512,4,128]{1,3,2,0:T(8,128)S(1)} fusion(bf16[4,128,8192]{2,1,0:T(8,128)(2,1)} %bitcast.91, bf16[1,512,8192]{2,1,0:T(8,128)(2,1)S(1)} %copy-done), kind=kOutput, calls=%fused_computation.23 | convolution fusion | flops 4294967296 | bytes 17825792 | tf_op jit(solution)/shard_map/dot_general | solution.py:102
  674.3 0.2 fusion.43
  674.5 0.9 fusion.7
  675.4 2.0 copy-done.1
  677.4 0.9 fusion.6
  678.3 9.0 %fusion.17 = bf16[128,4,512]{2,0,1:T(8,128)(2,1)S(1)} fusion(f32[4,512]{1,0:T(4,128)S(1)} %fusion.6, f32[4,512]{1,0:T(4,128)S(1)} %get-tuple-element.26, f32[512,512,4]{1,0,2:T(8,128)} %copy-done.1, pred[512,512]{0,1:T(8,128)(4,1)S(1)} %iota_compare_fusion, bf16[8192,768]{1,0:T(8,128)(2,1)} %all-gather.6.cloned.1.call-done, ...), kind=kOutput, calls=%fused_computation.24 | convolution fusion | flops 1347747840 | bytes 15482880 | tf_op jit(solution)/shard_map/while/body/eval_jaxpr/kgst,tkd->skgd/dot_general | solution.py:76
  687.2 1.0 copy.26
  (18 shorter events, 0.1 us)
Async XLA Ops:
  7.4 251.9 %all-reduce.3.cloned.1.call-start = ((), (), s32[]{:S(2)}) async-start(), calls=%async_computation.7 | async-start | bytes 131072
  8.1 0.6 copy-start.3
  8.8 413.7 %reduce-scatter.3.cloned.1.call-start = ((), (), s32[]{:S(2)}) async-start(), calls=%async_computation.3 | async-start | bytes 10485760 | tf_op jit(solution)/shard_map/reduce_scatter | solution.py:20
  343.1 79.5 %copy-start.2 = (bf16[256,512]{1,0:T(8,128)(2,1)S(1)}, bf16[256,512]{1,0:T(8,128)(2,1)}, u32[]{:S(2)}) copy-start(bf16[256,512]{1,0:T(8,128)(2,1)} %param.9) | copy-start | bytes 786436
  343.1 79.5 %copy-start.4 = (bf16[256,128]{1,0:T(8,128)(2,1)S(1)}, bf16[256,128]{1,0:T(8,128)(2,1)}, u32[]{:S(2)}) copy-start(bf16[256,128]{1,0:T(8,128)(2,1)} %param.11) | copy-start | bytes 196612
  343.1 79.5 %copy-start.5 = (bf16[256,128]{1,0:T(8,128)(2,1)S(1)}, bf16[256,128]{1,0:T(8,128)(2,1)}, u32[]{:S(2)}) copy-start(bf16[256,128]{1,0:T(8,128)(2,1)} %param.10) | copy-start | bytes 196612
  343.1 128.3 %copy-start.6 = (bf16[8192]{0:T(1024)(128)(2,1)S(1)}, bf16[8192]{0:T(1024)(128)(2,1)}, u32[]{:S(2)}) copy-start(bf16[8192]{0:T(1024)(128)(2,1)} %param.8) | copy-start | bytes 49156
  343.1 120.0 %reduce-scatter.5.cloned.1.call-start = ((), (), s32[]{:S(2)}) async-start(), calls=%async_computation.4 | async-start | bytes 3145728 | tf_op jit(solution)/shard_map/reduce_scatter | solution.py:20
  422.5 124.7 %all-gather.6.cloned.1.call-start = ((), (), s32[]{:S(2)}) async-start(), calls=%async_computation.6 | async-start | bytes 12976128 | tf_op jit(solution)/shard_map/all_gather | solution.py:37
  463.1 45.5 %all-to-all-start = ((bf16[32,1,1,64,256]{4,3,2,1,0:T(8,128)(2,1)}), bf16[32,1,1,64,256]{4,3,2,1,0:T(8,128)(2,1)S(1)}, u32[]{:S(2)}, u32[]{:S(2)}) async-start(bf16[32,1,1,64,256]{4,3,2,1,0:T(8,128)(2,1)} %bitcast.92), calls=%async_computation.2 | async-start | bytes 2097152 | tf_op jit(solution)/shard_map/all_to_all | solution.py:94
  471.1 188.4 %all-gather.4.cloned.1.call-start = ((), (), s32[]{:S(2)}) async-start(), calls=%async_computation.5 | async-start | bytes 9437184 | tf_op jit(solution)/shard_map/all_gather | solution.py:98
  659.5 7.6 %copy-start = (bf16[1,512,8192]{2,1,0:T(8,128)(2,1)S(1)}, bf16[1,512,8192]{2,1,0:T(8,128)(2,1)}, u32[]{:S(2)}) copy-start(bf16[1,512,8192]{2,1,0:T(8,128)(2,1)} %all-gather.4.cloned.1.call-done) | copy-start | bytes 25165828
  675.4 2.0 copy-start.1
Sparse Core Ops, SparseCore 0:
  13.7 245.6 all-reduce.2
  343.2 79.1 reduce-scatter.2
  425.0 38.1 reduce-scatter.4
Sparse Core Ops, SparseCore 1:
  424.8 122.3 all-gather.5
  549.7 109.7 all-gather.3
where the time goes:
time: 696 us; the launch traced here: 695 us
  waiting for transfers between devices  532 us (76%)
  local copies, waits for them, and re-layouts  102 us (15%)
  matrix products  24 us (3%)
  between operations  14.8 us (2%)
  other arithmetic  14.3 us (2%)
  starting transfers between devices  8.37 us (1%)
    unnamed x6, waiting for transfers between devices  251 us
    reduce_scatter x2, waiting for transfers between devices, reduced_to_own(): tiles = lax.psum_scatter(tiles, axes[k], scatter_dimension=0, tiled=True)  119 us
    all_gather x1, waiting for transfers between devices, per_device(): normed = lax.all_gather(share_normed, MP, axis=1, tiled=True)  93 us
    gather x1, local copies, waits for them, and re-layouts, per_device(): looked = jnp.take(embedding, jnp.clip(local_ids, 0, vocab_rows - 1), axis=0)  65.6 us
    all_to_all x1, waiting for transfers between devices, per_device(): lax.all_to_all(shared.astype(jnp.bfloat16), 'dp', split_axis=0, concat_ax...  37.2 us
    all_gather x1, waiting for transfers between devices, side_by_side(): whole, at, outs = (lax.all_gather(both, axis, axis=dim, tiled=True), 0, [])  31.8 us
    dot_general x2, local copies, waits for them, and re-layouts, project(): return jnp.dot(flat_normed, piece, preferred_element_type=jnp.float32)  19.4 us
    dot_general x2, matrix products, project(): return jnp.dot(flat_normed, piece, preferred_element_type=jnp.float32)  14.2 us
  transfers between devices with their start and end apart: 6, of which 6 were waited for; matrix products, arithmetic and copies ran while one was open for 4% of the time, Pallas kernels for 0%

commit v1 on v0

--- a/solution.py
+++ b/solution.py
@@ -95,7 +95,9 @@
         shared.astype(jnp.bfloat16), "dp", split_axis=0, concat_axis=4, tiled=True
     )
     share_normed = normalize(moved.astype(jnp.float32).reshape(responses, span, -1), norm_gain)
-    normed = lax.all_gather(share_normed, MP, axis=1, tiled=True)
+    normed = jnp.concatenate(
+        lax.all_to_all(jnp.stack([share_normed] * lax.axis_size(MP)), MP, 0, 0), axis=1
+    )
     flat_normed = normed.reshape(responses * length, -1)
 
     def project(piece):

time: 696 us -> 670 us (0.963)
  waiting for transfers between devices: 532 us -> 503 us
    all_gather x1 -> x0, waiting for transfers between devices: 93 us -> none  [per_device(): normed = lax.all_gather(share_normed, MP, axis=1, tiled=True)]
    all_to_all x0 -> x1, waiting for transfers between devices: none -> 47.2 us  [per_device(): lax.all_to_all(jnp.stack([share_normed] * lax.axis_size(MP)), MP, 0, 0)]
    all_gather x1, waiting for transfers between devices: 31.8 us -> 48.2 us  [side_by_side(): whole, at, outs = (lax.all_gather(both, axis, axis=dim, tiled=True), 0, [])]
    reshape x1 -> x0, local copies, waits for them, and re-layouts: 8.28 us -> none  [reduced_to_own(): tiles = tiles.reshape(*shape, *tiles.shape[1:])]
    transpose x0 -> x1, local copies, waits for them, and re-layouts: none -> 8.27 us  [reduced_to_own(): tiles = tiles.transpose(*order, *range(len(axes), tiles.ndim))]
    unnamed x6 -> x5, waiting for transfers between devices: 251 us -> 251 us
where the time goes in v1:
time: 670 us; the launch traced here: 669 us
  waiting for transfers between devices  503 us (75%)
  local copies, waits for them, and re-layouts  101 us (15%)
  matrix products  23.9 us (4%)
  between operations  14.8 us (2%)
  other arithmetic  13.6 us (2%)
  starting transfers between devices  13.4 us (2%)
    unnamed x5, waiting for transfers between devices  251 us
    reduce_scatter x2, waiting for transfers between devices, reduced_to_own(): tiles = lax.psum_scatter(tiles, axes[k], scatter_dimension=0, tiled=True)  119 us
    gather x1, local copies, waits for them, and re-layouts, per_device(): looked = jnp.take(embedding, jnp.clip(local_ids, 0, vocab_rows - 1), axis=0)  65.3 us
    all_gather x1, waiting for transfers between devices, side_by_side(): whole, at, outs = (lax.all_gather(both, axis, axis=dim, tiled=True), 0, [])  48.2 us
    all_to_all x1, waiting for transfers between devices, per_device(): lax.all_to_all(jnp.stack([share_normed] * lax.axis_size(MP)), MP, 0, 0)  47.2 us
    all_to_all x1, waiting for transfers between devices, per_device(): lax.all_to_all(shared.astype(jnp.bfloat16), 'dp', split_axis=0, concat_ax...  37.5 us
    dot_general x2, local copies, waits for them, and re-layouts, project(): return jnp.dot(flat_normed, piece, preferred_element_type=jnp.float32)  18.5 us
    dot_general x2, matrix products, project(): return jnp.dot(flat_normed, piece, preferred_element_type=jnp.float32)  14 us
  transfers between devices with their start and end apart: 6, of which 6 were waited for; matrix products, arithmetic and copies ran while one was open for 4% of the time, Pallas kernels for 0%

profile of v1, /device:TPU:1, one launch (start us, length us, event | category | flops | bytes accessed | tf_op | source)
XLA Modules:
  0.0 669.3 jit_solution(4049865172269378951)
XLA Ops:
  7.4 0.8 bitcast_dynamic-update-slice_fusion
  8.1 0.6 copy-done.3
  8.8 0.0 all-reduce.3.cloned.1.call-update
  8.8 0.0 reduce-scatter.3.cloned.1.call-start
  8.9 250.5 %all-reduce.3.cloned.1.call-done = s32[16384]{0:T(1024)} async-done(((s32[16384]{0:T(1024)}), s32[16384]{0:T(1024)}) %all-reduce.3.cloned.1.call-update) | async-done | bytes 65552
  259.3 0.9 subtract_clamp_fusion
  260.2 0.1 min.18
  260.3 0.1 min.16
  260.4 0.1 reshape.353
  260.6 0.9 compare_and_fusion.1
  261.4 0.1 and.23
  261.5 65.3 %gather_fusion = bf16[16384,256]{1,0:T(8,128)(2,1)} fusion(bf16[16032,256]{1,0:T(8,128)(2,1)} %param.7, s32[16384]{0:T(1024)S(1)} %broadcast_clamp_fusion), kind=kCustom, calls=%fused_computation | custom fusion | bytes 16842752 | tf_op jit(solution)/shard_map/jit(_take)/gather | solution.py:91
  326.8 7.8 %fusion = bf16[32,1,8,1,64,256]{5,4,0,2,3,1:T(8,128)(2,1)} fusion(bf16[32,1,8,1,64,256]{5,4,2,0,3,1:T(8,128)(2,1)} %bitcast.83, pred[32,8,64]{2,0,1:T(8,128)(4,1)S(1)} %copy.38, pred[32,8,64]{2,0,1:T(8,128)(4,1)S(1)} %copy.37), kind=kLoop, calls=%fused_computation.3 | loop fusion | flops 8388608 | bytes 16809984 | tf_op jit(solution)/shard_map/jit(_where)/select_n | solution.py:92
  334.6 8.3 %copy.40 = bf16[4,2,32,1,1,64,256]{6,5,2,1,0,4,3:T(8,128)(2,1)} copy(bf16[4,2,32,1,1,64,256]{6,5,2,0,1,4,3:T(8,128)(2,1)} %bitcast.85) | data formatting | bytes 16777216 | tf_op jit(solution)/shard_map/transpose | solution.py:17
  342.9 0.0 reduce-scatter.3.cloned.1.call-update
  342.9 0.0 copy-start.6
  343.0 0.0 reduce-scatter.5.cloned.1.call-start
  343.0 79.3 %reduce-scatter.3.cloned.1.call-done = bf16[2,32,1,1,64,256]{5,4,1,0,3,2:T(8,128)(2,1)} async-done(((bf16[8,32,1,1,64,256]{5,4,1,0,3,2:T(8,128)(2,1)}), bf16[2,32,1,1,64,256]{5,4,1,0,3,2:T(8,128)(2,1)}) %reduce-scatter.3.cloned.1.call-update) | async-done | bytes 2097168 | tf_op jit(solution)/shard_map/reduce_scatter | solution.py:20
  422.3 0.0 reduce-scatter.5.cloned.1.call-update
  422.3 0.0 all-gather.3.cloned.1.call-start
  422.4 0.8 pad_maximum_fusion
  423.2 0.0 all-gather.3.cloned.1.call-update
  423.2 39.8 %reduce-scatter.5.cloned.1.call-done = bf16[1,32,1,1,64,256]{5,4,1,0,3,2:T(8,128)(2,1)} async-done(((bf16[2,32,1,1,64,256]{5,4,1,0,3,2:T(8,128)(2,1)}), bf16[1,32,1,1,64,256]{5,4,1,0,3,2:T(8,128)(2,1)}) %reduce-scatter.5.cloned.1.call-update) | async-done | bytes 1048592 | tf_op jit(solution)/shard_map/reduce_scatter | solution.py:20
  463.0 8.0 %all-to-all-start = ((bf16[32,1,1,64,256]{4,3,2,1,0:T(8,128)(2,1)}), bf16[32,1,1,64,256]{4,3,2,1,0:T(8,128)(2,1)S(1)}, u32[]{:S(2)}, u32[]{:S(2)}) async-start(bf16[32,1,1,64,256]{4,3,2,1,0:T(8,128)(2,1)} %bitcast.88), calls=%async_computation.2 | async-start | bytes 2097152 | tf_op jit(solution)/shard_map/all_to_all | solution.py:94
  471.0 0.0 copy-done.6
  471.0 37.5 %all-to-all-done = bf16[32,1,1,64,256]{4,3,2,1,0:T(8,128)(2,1)S(1)} async-done(((bf16[32,1,1,64,256]{4,3,2,1,0:T(8,128)(2,1)}), bf16[32,1,1,64,256]{4,3,2,1,0:T(8,128)(2,1)S(1)}, u32[]{:S(2)}, u32[]{:S(2)}) %all-to-all-start) | async-done | bytes 1048608 | tf_op jit(solution)/shard_map/all_to_all | solution.py:94
  508.5 0.3 fusion.42
  508.8 0.2 copy.55
  509.0 0.3 fusion.3
  509.3 0.3 multiply_convert_fusion
  509.6 4.3 stack.2
  513.9 5.2 all-to-all-start.1
  519.1 0.1 iota_compare_fusion
  519.2 0.5 fusion.34
  519.7 48.2 %all-gather.3.cloned.1.call-done = bf16[8192,768]{1,0:T(8,128)(2,1)} async-done(((bf16[256,768]{1,0:T(8,128)(2,1)}), bf16[8192,768]{1,0:T(8,128)(2,1)}) %all-gather.3.cloned.1.call-update) | async-done | bytes 12582928 | tf_op jit(solution)/shard_map/all_gather | solution.py:37
  568.0 7.1 %slice_bitcast_fusion = bf16[512,8192]{0,1:T(8,128)(2,1)} fusion(bf16[8192,768]{1,0:T(8,128)(2,1)} %all-gather.3.cloned.1.call-done), kind=kLoop, calls=%fused_computation.1 | loop fusion | bytes 16777216 | tf_op jit(solution)/shard_map/dot_general | solution.py:104
  575.1 11.3 %copy.43 = bf16[512,8192]{1,0:T(8,128)(2,1)} copy(bf16[512,8192]{0,1:T(8,128)(2,1)} %slice_bitcast_fusion) | data formatting | bytes 16777216 | tf_op jit(solution)/shard_map/dot_general | solution.py:104
  586.4 47.2 %all-to-all-done.1 = bf16[8,1,64,8192]{3,2,1,0:T(8,128)(2,1)} async-done(((bf16[8,1,64,8192]{3,2,1,0:T(8,128)(2,1)}), bf16[8,1,64,8192]{3,2,1,0:T(8,128)(2,1)}, u32[]{:S(2)}, u32[]{:S(2)}) %all-to-all-start.1) | async-done | bytes 8388640 | tf_op jit(solution)/shard_map/all_to_all | solution.py:99
  633.6 7.0 %fusion.14 = f32[1,512,1,128]{1,3,2,0:T(8,128)S(1)} fusion(bf16[512,8192]{1,0:T(8,128)(2,1)} %bitcast.10, bf16[8192,768]{1,0:T(8,128)(2,1)} %all-gather.3.cloned.1.call-done), kind=kOutput, calls=%fused_computation.22 | convolution fusion | flops 1073741824 | bytes 10747904 | tf_op jit(solution)/shard_map/dot_general | solution.py:104
  640.7 0.6 fusion.37
  641.2 7.0 %convolution_bitcast_fusion = f32[1,512,4,128]{1,3,2,0:T(8,128)S(1)} fusion(bf16[512,8192,1]{1,0,2:T(8,128)(2,1)} %bitcast.16, bf16[4,128,8192]{2,1,0:T(8,128)(2,1)S(1)} %bitcast.86), kind=kOutput, calls=%fused_computation.20 | convolution fusion | flops 4294967296 | bytes 17825792 | tf_op jit(solution)/shard_map/dot_general | solution.py:104
  648.3 0.2 fusion.29
  648.5 0.9 fusion.2
  649.3 0.0 copy-start.1
  649.4 2.0 copy-done.1
  651.3 0.9 fusion.1
  652.2 9.0 %fusion.11 = bf16[128,4,512]{2,0,1:T(8,128)(2,1)S(1)} fusion(f32[4,512]{1,0:T(4,128)S(1)} %fusion.1, f32[4,512]{1,0:T(4,128)S(1)} %get-tuple-element.26, f32[512,512,4]{1,0,2:T(8,128)} %copy-done.1, pred[512,512]{0,1:T(8,128)(4,1)S(1)} %iota_compare_fusion, bf16[512,8192]{1,0:T(8,128)(2,1)} %bitcast.10, bf16[8192,768]{1,0:T(8,128)(2,1)} %all-gather.3.cloned.1.call-done), kind=kOutput, calls=%fused_computation.21 | convolution fusion | flops 1347747840 | bytes 15482880 | tf_op jit(solution)/shard_map/while/body/eval_jaxpr/kgst,tkd->skgd/dot_general | solution.py:76
  661.2 1.0 copy.48
  (19 shorter events, 0.2 us)
Async XLA Ops:
  7.4 251.9 %all-reduce.3.cloned.1.call-start = ((), (), s32[]{:S(2)}) async-start(), calls=%async_computation.7 | async-start | bytes 131072
  8.1 0.6 copy-start.3
  8.8 413.5 %reduce-scatter.3.cloned.1.call-start = ((), (), s32[]{:S(2)}) async-start(), calls=%async_computation.4 | async-start | bytes 10485760 | tf_op jit(solution)/shard_map/reduce_scatter | solution.py:20
  342.9 79.5 %copy-start.2 = (bf16[256,512]{1,0:T(8,128)(2,1)S(1)}, bf16[256,512]{1,0:T(8,128)(2,1)}, u32[]{:S(2)}) copy-start(bf16[256,512]{1,0:T(8,128)(2,1)} %param.9) | copy-start | bytes 786436
  342.9 79.5 %copy-start.4 = (bf16[256,128]{1,0:T(8,128)(2,1)S(1)}, bf16[256,128]{1,0:T(8,128)(2,1)}, u32[]{:S(2)}) copy-start(bf16[256,128]{1,0:T(8,128)(2,1)} %param.11) | copy-start | bytes 196612
  342.9 79.5 %copy-start.5 = (bf16[256,128]{1,0:T(8,128)(2,1)S(1)}, bf16[256,128]{1,0:T(8,128)(2,1)}, u32[]{:S(2)}) copy-start(bf16[256,128]{1,0:T(8,128)(2,1)} %param.10) | copy-start | bytes 196612
  342.9 128.1 %copy-start.6 = (bf16[8192]{0:T(1024)(128)(2,1)S(1)}, bf16[8192]{0:T(1024)(128)(2,1)}, u32[]{:S(2)}) copy-start(bf16[8192]{0:T(1024)(128)(2,1)} %param.8) | copy-start | bytes 49156
  343.0 120.0 %reduce-scatter.5.cloned.1.call-start = ((), (), s32[]{:S(2)}) async-start(), calls=%async_computation.5 | async-start | bytes 3145728 | tf_op jit(solution)/shard_map/reduce_scatter | solution.py:20
  422.3 145.6 %all-gather.3.cloned.1.call-start = ((), (), s32[]{:S(2)}) async-start(), calls=%async_computation.6 | async-start | bytes 12976128 | tf_op jit(solution)/shard_map/all_gather | solution.py:37
  463.0 45.5 %all-to-all-start = ((bf16[32,1,1,64,256]{4,3,2,1,0:T(8,128)(2,1)}), bf16[32,1,1,64,256]{4,3,2,1,0:T(8,128)(2,1)S(1)}, u32[]{:S(2)}, u32[]{:S(2)}) async-start(bf16[32,1,1,64,256]{4,3,2,1,0:T(8,128)(2,1)} %bitcast.88), calls=%async_computation.2 | async-start | bytes 2097152 | tf_op jit(solution)/shard_map/all_to_all | solution.py:94
  513.9 119.8 %all-to-all-start.1 = ((bf16[8,1,64,8192]{3,2,1,0:T(8,128)(2,1)}), bf16[8,1,64,8192]{3,2,1,0:T(8,128)(2,1)}, u32[]{:S(2)}, u32[]{:S(2)}) async-start(bf16[8,1,64,8192]{3,2,1,0:T(8,128)(2,1)} %stack.2), calls=%async_computation.3 | async-start | bytes 16777216 | tf_op jit(solution)/shard_map/all_to_all | solution.py:99
  633.6 7.6 %copy-start = (bf16[512,8192]{1,0:T(8,128)(2,1)S(1)}, bf16[512,8192]{1,0:T(8,128)(2,1)}, u32[]{:S(2)}) copy-start(bf16[512,8192]{1,0:T(8,128)(2,1)} %copy.43) | copy-start | bytes 25165828
  649.3 2.0 copy-start.1
Sparse Core Ops, SparseCore 0:
  13.7 245.6 all-reduce.2
  343.1 79.1 reduce-scatter.2
  424.8 38.1 reduce-scatter.4
Sparse Core Ops, SparseCore 1:
  424.7 143.2 all-gather.2
